TPU v7x, 256 devices: a 8x8x2 block of a 8x8x16 slice. The times are simulated.
256 devices in a mesh: parts: 2 (over z), seq: 128 (over x, y, core).
Axes of the slice: x: 8, y: 8, z: 2, core: 2. Of those that a mesh axis runs over, the one named last changes fastest.
The devices are a block of a 8x8x16 slice.
Arguments:
- token_ids: int32 [4, 4], P(None, 'parts'), parts along dimension 1, may hold values from 0 to 76031
- lengths: int32 [4], P('parts'), parts along dimension 0, may hold values from 24576 to 32768, as said below
- embed_table: bfloat16 [76032, 5120], P('seq'), may hold values from -6 to 6
- attn_gain: bfloat16 [5120], replicated, may hold values from 0.25 to 1.75
- w_qkv: bfloat16 [5120, 7168], P('seq'), may hold values from -0.3125 to 0.3125
- qkv_bias: float32 [7168], replicated, may hold values from -8 to 8
- cache_keys: bfloat16 [4, 32768, 1024], P('parts', 'seq'), parts along dimension 0, may hold values from -300 to 300
- cache_values: bfloat16 [4, 32768, 1024], P('parts', 'seq'), parts along dimension 0, may hold values from -6 to 6
- w_out: bfloat16 [5120, 5120], P(None, 'seq'), may hold values from -0.078125 to 0.078125
- mlp_gain: bfloat16 [5120], replicated, may hold values from 0.25 to 1.75
- w_gate: bfloat16 [5120, 16384], P(None, 'seq'), may hold values from -0.078125 to 0.078125
- w_up: bfloat16 [5120, 16384], P(None, 'seq'), may hold values from -0.078125 to 0.078125
- w_down: bfloat16 [16384, 5120], P('seq'), may hold values from -0.1875 to 0.1875
Outputs:
- attended: bfloat16 [4, 4, 5120], P(None, 'parts'), parts along dimension 1
- layer_out: bfloat16 [4, 4, 5120], P(None, 'parts', 'seq'), parts along dimension 1
There are 2 independent parts, one for each index of `parts`. A program takes and returns all parts, laid end to end along the dimension named above; an argument that names none is the same for every part. Nothing has to cross between parts.
Inputs may be any that keep to these rules, and one draw needn't show every extreme that they name: Cache positions lengths[b] and later are unused; the first prompt fills the whole cache of 32768 positions.
All inputs are finite; a program needn't handle non-finite values.
Results may differ from a plain program's by a relative error of at most 0.017.
The roundings to bfloat16 on the way count: a program that leaves them out, or rounds other values in their place, can miss the bound.
Values may be sent and summed in bfloat16 or wider, within the bound.
No kernel may reach another device: no remote copies, remote signals or barrier semaphores. Data moves between devices by JAX's collectives and lax.ppermute only.
A program may use at most 128 MiB of HBM per device.

v0:
```python
import math
import jax
import jax.numpy as jnp
from jax import lax
from jax.sharding import Mesh
from jax.sharding import PartitionSpec as P

HEADS = 40
KV_HEADS = 8
HEAD_DIM = 128
SEQ = ("seq_0", "seq_1", "seq_2")
NORM_EPS = 1e-06
ROPE_BASE = 1000000.0
MASKED = -1e30


def gathered_once(array, axis):
    leaves = jax.tree.leaves(array)
    order = sorted(range(len(leaves)), key=lambda k: -leaves[k].size)
    width = (1, *leaves[order[0]].shape)[-1]
    lines = [
        jnp.pad(leaves[k].reshape(-1), (0, -leaves[k].size % width)).reshape(-1, width)
        for k in order
    ]
    both, at, found = (lax.all_gather(jnp.concatenate(lines), axis), 0, {})
    for k, line in zip(order, lines):
        slab = both[:, at : at + len(line)].reshape(len(both), -1)
        found[k] = slab[:, : leaves[k].size].reshape(-1, *leaves[k].shape)
        at += len(line)
    numbers = iter(range(len(leaves)))
    return jax.tree.map(lambda _: found[next(numbers)], array)


def combined_by_axis(array, axes, combine):
    for axis in axes:
        pieces = gathered_once(array, axis)
        array = jax.tree.map(lambda part: part[0], pieces)
        for k in range(1, lax.axis_size(axis)):
            array = combine(array, jax.tree.map(lambda part: part[k], pieces))
    return array


def sum_in_order(parts, axes, order):
    dims = [lax.axis_size(a) for a in axes]
    parts = parts.reshape(*dims, *parts.shape[1:])
    parts = parts.transpose(*order, *range(len(axes), parts.ndim))
    parts = parts.reshape(-1, *parts.shape[len(axes) :])
    for k in order:
        parts = lax.psum_scatter(parts, axes[k], scatter_dimension=0, tiled=True)
    return parts[0]


def cut_along(array, dim, devices):
    before, after = (array.shape[:dim], array.shape[dim + 1 :])
    return jnp.moveaxis(array.reshape(*before, devices, -1, *after), dim, 0)


def scatter_axes(array, axes, order, dim):
    devices = lax.axis_size(axes)
    return sum_in_order(cut_along(array, dim, devices), axes, order)


def rms_normalize(rows, gain):
    mean_square = jnp.mean(rows * rows, axis=-1, keepdims=True)
    return (rows * lax.rsqrt(mean_square + NORM_EPS) * gain.astype(jnp.float32)).astype(
        jnp.bfloat16
    )


def rotate(vectors, positions):
    half_dim = vectors.shape[-1] // 2
    frequency = ROPE_BASE ** (-2.0 * jnp.arange(half_dim, dtype=jnp.float32) / vectors.shape[-1])
    angles = positions.astype(jnp.float32)[..., None, None] * frequency
    cosine = jnp.cos(angles)
    sine_part = jnp.sin(angles)
    widened = vectors.astype(jnp.float32)
    first_half = widened[..., :half_dim]
    second = widened[..., half_dim:]
    joined = jnp.concatenate(
        [first_half * cosine - second * sine_part, second * cosine + first_half * sine_part],
        axis=-1,
    )
    return joined.astype(jnp.bfloat16)


def combine_partials(earlier, latter):
    top_one, total_one, sum_one = earlier
    top_two, total_two, sum_two = latter
    joined_top = jnp.maximum(top_one, top_two)
    scale_one = jnp.exp(top_one - joined_top)
    scale_two = jnp.exp(top_two - joined_top)
    return (
        joined_top,
        total_one * scale_one + total_two * scale_two,
        sum_one * scale_one[..., None] + sum_two * scale_two[..., None],
    )


def body(
    token_ids,
    lengths,
    embed_table,
    attn_gain,
    w_qkv,
    qkv_bias,
    cache_keys,
    cache_values,
    w_out,
    mlp_gain,
    w_gate,
    w_up,
    w_down,
):
    rank = lax.axis_index(SEQ)
    step_count, batch_count = token_ids.shape
    model_width = embed_table.shape[1]
    vocab_rows = embed_table.shape[0]
    query_width = HEADS * HEAD_DIM
    key_width = KV_HEADS * HEAD_DIM
    group_size = HEADS // KV_HEADS
    local_ids = token_ids - rank * vocab_rows
    inside = (local_ids >= 0) & (local_ids < vocab_rows)
    picked = jnp.take(embed_table, jnp.clip(local_ids, 0, vocab_rows - 1), axis=0)
    partial_rows = jnp.where(inside[..., None], picked.astype(jnp.float32), 0.0)
    stream = lax.psum(partial_rows, SEQ)
    normed = rms_normalize(stream, attn_gain).reshape(-1, model_width)
    feature_rows = w_qkv.shape[0]
    normed_local = lax.dynamic_slice_in_dim(normed, rank * feature_rows, feature_rows, 1)
    joint_partial = jnp.dot(normed_local, w_qkv, preferred_element_type=jnp.float32)
    joint_summed = lax.psum(joint_partial, SEQ)
    joint = (joint_summed + qkv_bias).astype(jnp.bfloat16).reshape(step_count, batch_count, -1)
    query_part = joint[..., :query_width].reshape(step_count, batch_count, HEADS, HEAD_DIM)
    key_part = joint[..., query_width : query_width + key_width].reshape(
        step_count, batch_count, KV_HEADS, HEAD_DIM
    )
    value_part = joint[..., query_width + key_width :].reshape(
        step_count, batch_count, KV_HEADS, HEAD_DIM
    )
    positions = lengths[None, :] + jnp.arange(step_count, dtype=jnp.int32)[:, None]
    queries = rotate(query_part, positions)
    new_keys = rotate(key_part, positions)
    grouped = queries.reshape(step_count, batch_count, KV_HEADS, group_size, HEAD_DIM)
    score_scale = 1.0 / math.sqrt(HEAD_DIM)
    local_len = cache_keys.shape[1]
    key_blocks = cache_keys.reshape(batch_count, local_len, KV_HEADS, HEAD_DIM)
    value_blocks = cache_values.reshape(batch_count, local_len, KV_HEADS, HEAD_DIM)
    scores = (
        jnp.einsum("sbkgd,bpkd->bkgsp", grouped, key_blocks, preferred_element_type=jnp.float32)
        * score_scale
    )
    places = rank * local_len + jnp.arange(local_len, dtype=jnp.int32)
    valid = (places[None, :] < lengths[:, None])[:, None, None, None, :]
    masked = jnp.where(valid, scores, MASKED)
    local_top = jnp.max(masked, axis=-1)
    weights = jnp.where(valid, jnp.exp(masked - local_top[..., None]), 0.0)
    local_total = jnp.sum(weights, axis=-1)
    local_sum = jnp.einsum(
        "bkgsp,bpkd->bkgsd",
        weights.astype(jnp.bfloat16),
        value_blocks,
        preferred_element_type=jnp.float32,
    )
    merged_top, merged_total, merged_sum = combined_by_axis(
        (local_top, local_total, local_sum), SEQ, combine_partials
    )
    new_scores = (
        jnp.einsum("sbkgd,tbkd->bkgst", grouped, new_keys, preferred_element_type=jnp.float32)
        * score_scale
    )
    step_index = jnp.arange(step_count, dtype=jnp.int32)
    causal = step_index[:, None] >= step_index[None, :]
    new_masked = jnp.where(causal, new_scores, MASKED)
    final_top = jnp.maximum(merged_top, jnp.max(new_masked, axis=-1))
    rescale = jnp.exp(merged_top - final_top)
    new_weights = jnp.where(causal, jnp.exp(new_masked - final_top[..., None]), 0.0)
    final_total = merged_total * rescale + jnp.sum(new_weights, axis=-1)
    final_sum = merged_sum * rescale[..., None] + jnp.einsum(
        "bkgst,tbkd->bkgsd",
        new_weights.astype(jnp.bfloat16),
        value_part,
        preferred_element_type=jnp.float32,
    )
    attended = jnp.transpose(final_sum / final_total[..., None], (3, 0, 1, 2, 4))
    attended = attended.reshape(step_count, batch_count, query_width).astype(jnp.bfloat16)
    shard_cols = w_out.shape[1]
    projected = jnp.dot(
        attended.reshape(-1, query_width), w_out, preferred_element_type=jnp.float32
    )
    stream_shard = lax.dynamic_slice_in_dim(stream, rank * shard_cols, shard_cols, 2)
    mid_shard = stream_shard + projected.reshape(step_count, batch_count, shard_cols)
    mid_rows = lax.all_gather(mid_shard, SEQ, axis=2, tiled=True)
    normed_mid = rms_normalize(mid_rows, mlp_gain)
    flat_rows = normed_mid.reshape(-1, model_width)
    gate = jnp.dot(flat_rows, w_gate, preferred_element_type=jnp.float32)
    upper = jnp.dot(flat_rows, w_up, preferred_element_type=jnp.float32)
    hidden = (jax.nn.silu(gate) * upper).astype(jnp.bfloat16)
    down_terms = jnp.dot(hidden, w_down, preferred_element_type=jnp.float32).reshape(
        step_count, batch_count, model_width
    )
    summed = scatter_axes(down_terms, SEQ, (2, 1, 0), 2)
    layer_out = (mid_shard + summed).astype(jnp.bfloat16)
    return (attended, layer_out)


def solution(mesh):
    finer = Mesh(
        mesh.devices.reshape(mesh.shape["parts"], 8, 8, 2), ("parts", "seq_0", "seq_1", "seq_2")
    )
    return jax.shard_map(
        body,
        mesh=finer,
        in_specs=(
            P(None, "parts"),
            P("parts"),
            P(SEQ, None),
            P(),
            P(SEQ, None),
            P(),
            P("parts", SEQ, None),
            P("parts", SEQ, None),
            P(None, SEQ),
            P(),
            P(None, SEQ),
            P(None, SEQ),
            P(SEQ, None),
        ),
        out_specs=(P(None, "parts", None), P(None, "parts", SEQ)),
        check_vma=False,
    )
```

profile of v0, /device:TPU:528, one launch (start us, length us, event | category | flops | bytes accessed | tf_op | source)
XLA Modules:
  0.0 717.2 jit_solution(17745230185070453889)
XLA Ops:
  8.3 4.2 gather_fusion
  14.4 1.1 copy-done.3
  15.8 1.1 bitcast_bitcast_fusion
  16.9 195.6 %all-reduce.14.cloned.1.call-done = f32[4,2,5120]{2,1,0:T(2,128)} async-done(((f32[4,2,5120]{2,1,0:T(2,128)}), f32[4,2,5120]{2,1,0:T(2,128)}) %all-reduce.14.cloned.1.call-update) | async-done | bytes 163856 | tf_op jit(solution)/shard_map/psum | solution.py:125
  212.4 1.1 multiply_reduce_fusion.1
  213.5 1.1 multiply_convert_fusion.1
  214.6 1.0 fusion.77
  215.8 181.4 %all-reduce.16.cloned.1.call-done = f32[8,7168]{1,0:T(8,128)} async-done(((f32[8,7168]{1,0:T(8,128)}), f32[8,7168]{1,0:T(8,128)}) %all-reduce.16.cloned.1.call-update) | async-done | bytes 229392 | tf_op jit(solution)/shard_map/psum | solution.py:130
  397.2 1.0 add_convert_fusion
  400.1 1.5 fusion.9
  402.4 38.6 %all-gather.9.cloned.1.call-done = f32[8,326,128]{2,1,0:T(8,128)} async-done(((f32[1,326,128]{2,1,0:T(8,128)}), f32[8,326,128]{2,1,0:T(8,128)}) %all-gather.9.cloned.1.call-update) | async-done | bytes 1335312 | tf_op jit(solution)/shard_map/all_gather | solution.py:25
  442.1 2.0 fusion.39
  446.0 38.5 %all-gather.11.cloned.1.call-done = f32[8,326,128]{2,1,0:T(8,128)} async-done(((f32[1,326,128]{2,1,0:T(8,128)}), f32[8,326,128]{2,1,0:T(8,128)}) %all-gather.11.cloned.1.call-update) | async-done | bytes 1335312 | tf_op jit(solution)/shard_map/all_gather | solution.py:25
  485.6 2.0 fusion.18
  487.6 2.1 all-gather.5
  493.9 56.9 %all_gather.27 = f32[4,2,5120]{0,1,2:T(2,128)} all-gather(f32[4,2,40]{0,1,2:T(2,128)S(1)} %copy.230), channel_id=1, replica_groups=mesh['parts'=2,'seq_0'=8,'seq_1'=8,'seq_2'=2] {'seq_0','seq_1','seq_2'}, dimensions={2}, use_global_device_ids=true | all-gather | bytes 165120 | tf_op jit(solution)/shard_map/all_gather | solution.py:191
  550.8 5.6 copy.233
  556.5 7.0 multiply_reduce_fusion
  564.2 1.9 fusion.8
  566.7 1.1 copy.236
  569.3 30.1 %all-reduce.18.cloned.1.call-done = f32[128,4,2,40]{3,1,2,0:T(4,128)} async-done(((f32[128,4,2,40]{3,1,2,0:T(4,128)}), f32[128,4,2,40]{3,1,2,0:T(4,128)}) %all-reduce.18.cloned.1.call-update) | async-done | bytes 163856
  599.4 1.7 constant_dynamic-slice_fusion.2
  603.0 75.6 %all-reduce.20.cloned.1.call-done = f32[64,4,2,40]{3,1,2,0:T(4,128)} async-done(((f32[64,4,2,40]{3,1,2,0:T(4,128)}), f32[64,4,2,40]{3,1,2,0:T(4,128)}) %all-reduce.20.cloned.1.call-update) | async-done | bytes 81936
  679.4 29.7 %all-reduce.8 = f32[8,4,2,40]{3,1,2,0:T(4,128)S(1)} all-reduce(f32[8,4,2,40]{3,1,2,0:T(4,128)S(1)} %constant_dynamic-slice_fusion.1), channel_id=7, replica_groups=mesh['parts'=2,'seq_0'=8,'seq_1'=8,'seq_2'=2] {'seq_0'}, use_global_device_ids=true, to_apply=%region_10.11.clone | all-reduce | flops 2560 | bytes 20480
  (145 shorter events, 19.3 us)
Async XLA Ops:
  7.2 557.1 %copy-start = (bf16[128,5120]{1,0:T(8,128)(2,1)S(1)}, bf16[128,5120]{1,0:T(8,128)(2,1)}, u32[]{:S(2)}) copy-start(bf16[128,5120]{1,0:T(8,128)(2,1)} %param.25) | copy-start | bytes 3932164
  7.2 6.6 copy-start.7
  7.2 6.6 copy-start.9
  7.2 6.8 copy-start.2
  7.2 205.2 %all-reduce.14.cloned.1.call-start = ((), (), s32[]{:S(2)}) async-start(), calls=%async_computation | async-start | bytes 327680 | tf_op jit(solution)/shard_map/psum | solution.py:125
  13.7 383.5 %all-reduce.16.cloned.1.call-start = ((), (), s32[]{:S(2)}) async-start(), calls=%async_computation.1 | async-start | bytes 458752 | tf_op jit(solution)/shard_map/psum | solution.py:130
  14.3 1.2 copy-start.3
  15.8 198.8 %copy-start.4 = (bf16[40,7168]{1,0:T(8,128)(2,1)S(1)}, bf16[40,7168]{1,0:T(8,128)(2,1)}, u32[]{:S(2)}) copy-start(bf16[40,7168]{1,0:T(8,128)(2,1)} %param.17) | copy-start | bytes 1720324
  16.9 380.3 %copy-start.6 = (f32[7168]{0:T(1024)S(1)}, f32[7168]{0:T(1024)}, u32[]{:S(2)}) copy-start(f32[7168]{0:T(1024)} %param.18) | copy-start | bytes 86020
  215.7 225.3 %all-gather.9.cloned.1.call-start = ((), (), s32[]{:S(2)}) async-start(), calls=%async_computation.2 | async-start | bytes 1511424 | tf_op jit(solution)/shard_map/all_gather | solution.py:25
  402.3 42.6 %copy-start.8 = (bf16[5120]{0:T(1024)(128)(2,1)S(1)}, bf16[5120]{0:T(1024)(128)(2,1)}, u32[]{:S(2)}) copy-start(bf16[5120]{0:T(1024)(128)(2,1)} %param.22) | copy-start | bytes 30724
  402.3 82.2 %all-gather.11.cloned.1.call-start = ((), (), s32[]{:S(2)}) async-start(), calls=%async_computation.3 | async-start | bytes 1511424 | tf_op jit(solution)/shard_map/all_gather | solution.py:25
  444.8 154.6 %all-reduce.18.cloned.1.call-start = ((), (), s32[]{:S(2)}) async-start(), calls=%async_computation.4 | async-start | bytes 1048576
  491.8 1.0 copy-start.10
  492.8 58.0 %copy-start.5 = (bf16[4,2,5120]{2,1,0:T(2,128)(2,1)}, bf16[4,2,5120]{2,1,0:T(2,128)(2,1)S(1)}, u32[]{:S(2)}) copy-start(bf16[4,2,5120]{2,1,0:T(2,128)(2,1)S(1)} %convert_element_type.84) | copy-start | bytes 245764
  556.5 7.5 %copy-start.1 = (bf16[5120,128]{1,0:T(8,128)(2,1)S(1)}, bf16[5120,128]{1,0:T(8,128)(2,1)}, u32[]{:S(2)}) copy-start(bf16[5120,128]{1,0:T(8,128)(2,1)} %param.23) | copy-start | bytes 3932164
  566.5 1.5 copy-start.13
  566.7 34.4 %copy-start.12 = (u32[256]{0:T(256)S(1)}, u32[256]{0:T(256)}, u32[]{:S(2)}) copy-start(u32[256]{0:T(256)} %constant.90) | copy-start | bytes 3076
  566.7 35.0 %copy-start.11 = (u32[256]{0:T(256)S(1)}, u32[256]{0:T(256)}, u32[]{:S(2)}) copy-start(u32[256]{0:T(256)} %constant.94) | copy-start | bytes 3076
  567.9 110.7 %all-reduce.20.cloned.1.call-start = ((), (), s32[]{:S(2)}) async-start(), calls=%async_computation.5 | async-start | bytes 524288
Sparse Core Ops, SparseCore 0:
  13.8 198.6 all-reduce.13
  215.8 181.3 all-reduce.15
  402.5 38.5 all-gather.8
  444.9 39.5 all-gather.10
  568.1 31.3 all-reduce.17
  601.6 77.0 all-reduce.19
where the time goes:
time: 718 us; the launch traced here: 717 us
  waiting for transfers between devices  560 us (78%)
  blocking collectives  88.7 us (12%)
  local copies, waits for them, and re-layouts  25.4 us (4%)
  other arithmetic  19.2 us (3%)
  between operations  16 us (2%)
  matrix products  7.37 us (1%)
    psum x1, waiting for transfers between devices, body(): stream = lax.psum(partial_rows, SEQ)  196 us
    psum x1, waiting for transfers between devices, body(): joint_summed = lax.psum(joint_partial, SEQ)  181 us
    unnamed x8, waiting for transfers between devices  106 us
    all_gather x2, waiting for transfers between devices, gathered_once(): both, at, found = (lax.all_gather(jnp.concatenate(lines), axis), 0, {})  77.1 us
    all_gather x1, blocking collectives, body(): mid_rows = lax.all_gather(mid_shard, SEQ, axis=2, tiled=True)  56.9 us
    unnamed x1, blocking collectives  29.7 us
  transfers between devices with their start and end apart: 6, of which 6 were waited for; matrix products, arithmetic and copies ran while one was open for 1% of the time, Pallas kernels for 0%

commit v1 on v0

--- a/solution.py
+++ b/solution.py
@@ -127,7 +127,8 @@
     feature_rows = w_qkv.shape[0]
     normed_local = lax.dynamic_slice_in_dim(normed, rank * feature_rows, feature_rows, 1)
     joint_partial = jnp.dot(normed_local, w_qkv, preferred_element_type=jnp.float32)
-    joint_summed = lax.psum(joint_partial, SEQ)
+    shards = lax.all_gather(joint_partial, SEQ)
+    joint_summed = jnp.sum(shards, axis=0)
     joint = (joint_summed + qkv_bias).astype(jnp.bfloat16).reshape(step_count, batch_count, -1)
     query_part = joint[..., :query_width].reshape(step_count, batch_count, HEADS, HEAD_DIM)
     key_part = joint[..., query_width : query_width + key_width].reshape(

time: 718 us -> 671 us (0.935)
  waiting for transfers between devices: 560 us -> 504 us
  other arithmetic: 19.2 us -> 28.9 us
    psum x1 -> x0, waiting for transfers between devices: 181 us -> none  [body(): joint_summed = lax.psum(joint_partial, SEQ)]
    all_gather x0 -> x1, waiting for transfers between devices: none -> 121 us  [body(): shards = lax.all_gather(joint_partial, SEQ)]
    reduce_sum x0 -> x1, other arithmetic: none -> 10.6 us  [body(): joint_summed = jnp.sum(shards, axis=0)]
where the time goes in v1:
time: 671 us; the launch traced here: 670 us
  waiting for transfers between devices  504 us (75%)
  blocking collectives  88.7 us (13%)
  other arithmetic  28.9 us (4%)
  local copies, waits for them, and re-layouts  25 us (4%)
  between operations  16 us (2%)
  matrix products  7.37 us (1%)
    psum x1, waiting for transfers between devices, body(): stream = lax.psum(partial_rows, SEQ)  199 us
    all_gather x1, waiting for transfers between devices, body(): shards = lax.all_gather(joint_partial, SEQ)  121 us
    unnamed x8, waiting for transfers between devices  106 us
    all_gather x2, waiting for transfers between devices, gathered_once(): both, at, found = (lax.all_gather(jnp.concatenate(lines), axis), 0, {})  78 us
    all_gather x1, blocking collectives, body(): mid_rows = lax.all_gather(mid_shard, SEQ, axis=2, tiled=True)  56.9 us
    unnamed x1, blocking collectives  29.7 us
  transfers between devices with their start and end apart: 6, of which 6 were waited for; matrix products, arithmetic and copies ran while one was open for 1% of the time, Pallas kernels for 0%

profile of v1, /device:TPU:528, one launch (start us, length us, event | category | flops | bytes accessed | tf_op | source)
XLA Modules:
  0.0 669.9 jit_solution(16616535544786436360)
XLA Ops:
  8.3 4.3 gather_fusion
  13.8 198.7 %all-reduce.13.cloned.1.call-done = f32[4,2,5120]{2,1,0:T(2,128)} async-done(((f32[4,2,5120]{2,1,0:T(2,128)}), f32[4,2,5120]{2,1,0:T(2,128)}) %all-reduce.13.cloned.1.call-update) | async-done | bytes 163856 | tf_op jit(solution)/shard_map/psum | solution.py:125
  212.5 1.1 multiply_reduce_fusion.1
  213.6 1.1 multiply_convert_fusion.1
  214.7 1.0 fusion.77
  217.4 1.1 bitcast_bitcast_fusion
  218.5 120.8 %all-gather.11.cloned.1.call-done = f32[1024,7168]{1,0:T(8,128)} async-done(((f32[8,7168]{1,0:T(8,128)}), f32[1024,7168]{1,0:T(8,128)}) %all-gather.11.cloned.1.call-update) | async-done | bytes 29360144 | tf_op jit(solution)/shard_map/all_gather | solution.py:130
  339.2 10.6 %bitcast_reduce_fusion = f32[8,7168]{1,0:T(8,128)S(1)} fusion(f32[1024,7168]{1,0:T(8,128)} %all-gather.11.cloned.1.call-done), kind=kLoop, calls=%fused_computation.1 | loop fusion | flops 7282688 | bytes 29589504 | tf_op jit(solution)/shard_map/reduce_sum | solution.py:131
  351.9 1.5 fusion.9
  354.3 39.5 %all-gather.13.cloned.1.call-done = f32[8,326,128]{2,1,0:T(8,128)} async-done(((f32[1,326,128]{2,1,0:T(8,128)}), f32[8,326,128]{2,1,0:T(8,128)}) %all-gather.13.cloned.1.call-update) | async-done | bytes 1335312 | tf_op jit(solution)/shard_map/all_gather | solution.py:25
  394.8 2.0 fusion.39
  398.8 38.5 %all-gather.15.cloned.1.call-done = f32[8,326,128]{2,1,0:T(8,128)} async-done(((f32[1,326,128]{2,1,0:T(8,128)}), f32[8,326,128]{2,1,0:T(8,128)}) %all-gather.15.cloned.1.call-update) | async-done | bytes 1335312 | tf_op jit(solution)/shard_map/all_gather | solution.py:25
  438.3 2.0 fusion.18
  440.3 2.1 all-gather.6
  445.5 1.0 convolution_add_fusion.1
  446.6 56.9 %all_gather.35 = f32[4,2,5120]{0,1,2:T(2,128)} all-gather(f32[4,2,40]{0,1,2:T(2,128)S(1)} %copy.230), channel_id=1, replica_groups=mesh['parts'=2,'seq_0'=8,'seq_1'=8,'seq_2'=2] {'seq_0','seq_1','seq_2'}, dimensions={2}, use_global_device_ids=true | all-gather | bytes 165120 | tf_op jit(solution)/shard_map/all_gather | solution.py:192
  503.6 5.6 copy.233
  509.2 7.0 %multiply_reduce_fusion = f32[4,2]{0,1:T(2,128)S(1)} fusion(f32[4,2,5120]{0,1,2:T(2,128)} %all_gather.35), kind=kLoop, calls=%fused_computation.2 | loop fusion | flops 81912 | bytes 163872 | tf_op jit(solution)/shard_map/reduce_sum | solution.py:64
  517.0 1.9 fusion.8
  519.5 1.1 copy.236
  522.0 30.1 %all-reduce.15.cloned.1.call-done = f32[128,4,2,40]{3,1,2,0:T(4,128)} async-done(((f32[128,4,2,40]{3,1,2,0:T(4,128)}), f32[128,4,2,40]{3,1,2,0:T(4,128)}) %all-reduce.15.cloned.1.call-update) | async-done | bytes 163856
  552.2 1.7 constant_dynamic-slice_fusion.2
  555.8 75.6 %all-reduce.17.cloned.1.call-done = f32[64,4,2,40]{3,1,2,0:T(4,128)} async-done(((f32[64,4,2,40]{3,1,2,0:T(4,128)}), f32[64,4,2,40]{3,1,2,0:T(4,128)}) %all-reduce.17.cloned.1.call-update) | async-done | bytes 81936
  632.2 29.7 %all-reduce.8 = f32[8,4,2,40]{3,1,2,0:T(4,128)S(1)} all-reduce(f32[8,4,2,40]{3,1,2,0:T(4,128)S(1)} %constant_dynamic-slice_fusion.1), channel_id=8, replica_groups=mesh['parts'=2,'seq_0'=8,'seq_1'=8,'seq_2'=2] {'seq_0'}, use_global_device_ids=true, to_apply=%region_10.11.clone | all-reduce | flops 2560 | bytes 20480
  (146 shorter events, 19.1 us)
Async XLA Ops:
  7.2 509.8 %copy-start = (bf16[128,5120]{1,0:T(8,128)(2,1)S(1)}, bf16[128,5120]{1,0:T(8,128)(2,1)}, u32[]{:S(2)}) copy-start(bf16[128,5120]{1,0:T(8,128)(2,1)} %param.25) | copy-start | bytes 3932164
  7.2 6.6 copy-start.7
  7.2 207.5 %copy-start.4 = (bf16[40,7168]{1,0:T(8,128)(2,1)S(1)}, bf16[40,7168]{1,0:T(8,128)(2,1)}, u32[]{:S(2)}) copy-start(bf16[40,7168]{1,0:T(8,128)(2,1)} %param.17) | copy-start | bytes 1720324
  7.2 205.3 %all-reduce.13.cloned.1.call-start = ((), (), s32[]{:S(2)}) async-start(), calls=%async_computation | async-start | bytes 327680 | tf_op jit(solution)/shard_map/psum | solution.py:125
  8.3 207.6 %copy-start.9 = (s32[2]{0:T(128)S(1)}, s32[2]{0:T(128)}, u32[]{:S(2)}) copy-start(s32[2]{0:T(128)} %param.14) | copy-start | bytes 28
  8.3 207.8 %copy-start.2 = (bf16[2,256,1024]{2,1,0:T(8,128)(2,1)S(1)}, bf16[2,256,1024]{2,1,0:T(8,128)(2,1)}, u32[]{:S(2)}) copy-start(bf16[2,256,1024]{2,1,0:T(8,128)(2,1)} %param.19) | copy-start | bytes 3145732
  13.7 325.5 %all-gather.11.cloned.1.call-start = ((), (), s32[]{:S(2)}) async-start(), calls=%async_computation.1 | async-start | bytes 29589504 | tf_op jit(solution)/shard_map/all_gather | solution.py:130
  215.7 1.2 copy-start.3
  215.8 178.0 %all-gather.13.cloned.1.call-start = ((), (), s32[]{:S(2)}) async-start(), calls=%async_computation.2 | async-start | bytes 1511424 | tf_op jit(solution)/shard_map/all_gather | solution.py:25
  218.5 131.5 %copy-start.6 = (f32[7168]{0:T(1024)S(1)}, f32[7168]{0:T(1024)}, u32[]{:S(2)}) copy-start(f32[7168]{0:T(1024)} %param.18) | copy-start | bytes 86020
  354.1 43.5 %copy-start.8 = (bf16[5120]{0:T(1024)(128)(2,1)S(1)}, bf16[5120]{0:T(1024)(128)(2,1)}, u32[]{:S(2)}) copy-start(bf16[5120]{0:T(1024)(128)(2,1)} %param.22) | copy-start | bytes 30724
  354.2 83.1 %all-gather.15.cloned.1.call-start = ((), (), s32[]{:S(2)}) async-start(), calls=%async_computation.3 | async-start | bytes 1511424 | tf_op jit(solution)/shard_map/all_gather | solution.py:25
  397.5 154.6 %all-reduce.15.cloned.1.call-start = ((), (), s32[]{:S(2)}) async-start(), calls=%async_computation.4 | async-start | bytes 1048576
  444.5 1.0 copy-start.10
  445.5 58.0 %copy-start.5 = (bf16[4,2,5120]{2,1,0:T(2,128)(2,1)}, bf16[4,2,5120]{2,1,0:T(2,128)(2,1)S(1)}, u32[]{:S(2)}) copy-start(bf16[4,2,5120]{2,1,0:T(2,128)(2,1)S(1)} %convert_element_type.85) | copy-start | bytes 245764
  509.2 7.5 %copy-start.1 = (bf16[5120,128]{1,0:T(8,128)(2,1)S(1)}, bf16[5120,128]{1,0:T(8,128)(2,1)}, u32[]{:S(2)}) copy-start(bf16[5120,128]{1,0:T(8,128)(2,1)} %param.23) | copy-start | bytes 3932164
  519.3 1.5 copy-start.13
  519.5 34.4 %copy-start.12 = (u32[256]{0:T(256)S(1)}, u32[256]{0:T(256)}, u32[]{:S(2)}) copy-start(u32[256]{0:T(256)} %constant.90) | copy-start | bytes 3076
  519.5 35.0 %copy-start.11 = (u32[256]{0:T(256)S(1)}, u32[256]{0:T(256)}, u32[]{:S(2)}) copy-start(u32[256]{0:T(256)} %constant.94) | copy-start | bytes 3076
  520.7 110.7 %all-reduce.17.cloned.1.call-start = ((), (), s32[]{:S(2)}) async-start(), calls=%async_computation.5 | async-start | bytes 524288
Sparse Core Ops, SparseCore 0:
  13.8 198.6 all-reduce.12
  215.9 123.3 all-gather.10
  354.3 39.3 all-gather.12
  397.7 39.5 all-gather.14
  520.8 31.3 all-reduce.14
  554.4 77.0 all-reduce.16
